TPU v7x, 32 devices: a whole 2x2x4 slice. The times are simulated.
32 devices in a mesh: strip: 8 (over z, x), seq: 4 (over y, core).
Axes of the slice: x: 2, y: 2, z: 4, core: 2. Of those that a mesh axis runs over, the one named last changes fastest.
Arguments:
- patches: bfloat16 [32, 536, 768], P('strip', 'seq'), may hold values from -6 to 6
- lengths: int32 [32], P('strip'), may hold values from 1 to 536, as said below
- script: int32 [32], P('strip'), may hold values from 0 to 3, as said below
- script_table: bfloat16 [4, 768], replicated, may hold values from -3 to 3
- gain_one: float32 [768], replicated, may hold values from 0.25 to 1.75
- bias_one: float32 [768], replicated, may hold values from -2 to 2
- qkv_weight: bfloat16 [768, 2304], replicated, may hold values from -0.3125 to 0.3125
- query_bias: float32 [768], replicated, may hold values from -3 to 3
- value_bias: float32 [768], replicated, may hold values from -3 to 3
- out_weight: bfloat16 [768, 768], replicated, may hold values from -0.875 to 0.875
- out_bias: float32 [768], replicated, may hold values from -3 to 3
- gain_two: float32 [768], replicated, may hold values from 0.25 to 1.75
- bias_two: float32 [768], replicated, may hold values from -2 to 2
- up_weight: bfloat16 [768, 3072], replicated, may hold values from -0.21875 to 0.21875
- up_bias: float32 [3072], replicated, may hold values from -3 to 3
- down_weight: bfloat16 [3072, 768], replicated, may hold values from -0.109375 to 0.109375
- down_bias: float32 [768], replicated, may hold values from -3 to 3
- cotangent: bfloat16 [32, 536, 768], P('strip', 'seq'), may hold values from -6 to 6
Outputs:
- layer_out: bfloat16 [32, 536, 768], P('strip', 'seq')
- grad_patches: bfloat16 [32, 536, 768], P('strip', 'seq')
- grad_table: float32 [768, 4], P(('strip', 'seq'))
- grad_gain_one: float32 [768], P(('strip', 'seq'))
- grad_bias_one: float32 [768], P(('strip', 'seq'))
- grad_qkv: float32 [768, 2304], P(('strip', 'seq'))
- grad_query_bias: float32 [768], P(('strip', 'seq'))
- grad_value_bias: float32 [768], P(('strip', 'seq'))
- grad_out_weight: float32 [768, 768], P(('strip', 'seq'))
- grad_out_bias: float32 [768], P(('strip', 'seq'))
- grad_gain_two: float32 [768], P(('strip', 'seq'))
- grad_bias_two: float32 [768], P(('strip', 'seq'))
- grad_up_weight: float32 [768, 3072], P(('strip', 'seq'))
- grad_up_bias: float32 [3072], P(('strip', 'seq'))
- grad_down_weight: float32 [3072, 768], P(('strip', 'seq'))
- grad_down_bias: float32 [768], P(('strip', 'seq'))
Inputs may be any that keep to these rules, and one draw needn't show every extreme that they name: The first lengths[s] patch slots of strip s are filled; some strip has all 536 filled. `script`: script ids never fall from one strip to the next.
All inputs are finite; a program needn't handle non-finite values.
Results may differ from a plain program's by a relative error of at most 0.013.
The roundings to bfloat16 on the way count: a program that leaves them out, or rounds other values in their place, can miss the bound.
Values may be sent and summed in bfloat16 or wider, within the bound.
A program may use at most 192 MiB of HBM per device.

v0:
```python
import jax
import jax.numpy as jnp
from jax import lax
from jax.sharding import PartitionSpec as P

HD = 64
epsilon = 1e-12


def normalize(hidden):
    centred = hidden - jnp.mean(hidden, axis=-1, keepdims=True)
    inverse = lax.rsqrt(jnp.mean(centred * centred, axis=-1, keepdims=True) + epsilon)
    return (centred * inverse, inverse)


def norm_back(upstream, gain, normed, inverse):
    scaled = upstream * gain
    return inverse * (
        scaled
        - jnp.mean(scaled, axis=-1, keepdims=True)
        - normed * jnp.mean(scaled * normed, axis=-1, keepdims=True)
    )


def weight_grad(inputs, upstream):
    return lax.dot_general(
        inputs, upstream, (((0,), (0,)), ((), ())), preferred_element_type=jnp.float32
    )


def input_grad(upstream, weight):
    return lax.dot_general(
        upstream, weight, (((1,), (1,)), ((), ())), preferred_element_type=jnp.float32
    )


def gelu_slope(upper):
    return (
        0.5 * (1.0 + lax.erf(upper * 0.7071067811865476))
        + upper * jnp.exp(-0.5 * upper * upper) * 0.3989422804014327
    )


def split_block(block):
    seq_len = block.shape[0]
    heads_here = block.shape[2] // HD
    return [block[:, member].reshape(seq_len, heads_here, HD) for member in range(3)]


def masked_logits(queries, key_rows, length):
    logits = jnp.einsum(
        "qhd,khd->hqk", queries, key_rows, preferred_element_type=jnp.float32
    ) * HD ** (-0.5)
    visible = jnp.arange(logits.shape[-1], dtype=jnp.int32) < length
    return jnp.where(visible[None, None, :], logits, -1000000000.0)


def attend_forward(item):
    block, length = item
    queries, key_rows, values = split_block(block)
    logits = masked_logits(queries, key_rows, length)
    highest = jnp.max(logits, axis=-1, keepdims=True)
    expanded = jnp.exp(logits - highest)
    totals = jnp.sum(expanded, axis=-1, keepdims=True)
    probs = (expanded / totals).astype(jnp.bfloat16)
    mixed = jnp.einsum("hqk,khd->qhd", probs, values, preferred_element_type=jnp.float32)
    mixed = mixed.astype(jnp.bfloat16).reshape(block.shape[0], block.shape[2])
    return (mixed, (highest + jnp.log(totals))[..., 0])


def attend_backward(item):
    block, log_total, grad_mixed, length = item
    queries, key_rows, values = split_block(block)
    logits = masked_logits(queries, key_rows, length)
    probs = jnp.exp(logits - log_total[..., None])
    grad_heads = grad_mixed.reshape(queries.shape)
    grad_values = jnp.einsum(
        "hqk,qhd->khd", probs.astype(jnp.bfloat16), grad_heads, preferred_element_type=jnp.float32
    )
    grad_probs = jnp.einsum("qhd,khd->hqk", grad_heads, values, preferred_element_type=jnp.float32)
    inner = jnp.sum(probs * grad_probs, axis=-1, keepdims=True)
    grad_logits = (probs * (grad_probs - inner)).astype(jnp.bfloat16)
    grad_queries = jnp.einsum(
        "hqk,khd->qhd", grad_logits, key_rows, preferred_element_type=jnp.float32
    ) * HD ** (-0.5)
    grad_keys = jnp.einsum(
        "hqk,qhd->khd", grad_logits, queries, preferred_element_type=jnp.float32
    ) * HD ** (-0.5)
    stacked = jnp.stack([grad_queries, grad_keys, grad_values], axis=1)
    return stacked.reshape(block.shape).astype(jnp.bfloat16)


def local(
    patches,
    lengths,
    script,
    script_table,
    gain_one,
    bias_one,
    qkv_weight,
    query_bias,
    value_bias,
    out_weight,
    out_bias,
    gain_two,
    bias_two,
    up_weight,
    up_bias,
    down_weight,
    down_bias,
    cotangent,
):
    strips, row_count, model_width = patches.shape
    groups = script_table.shape[0]
    tokens = strips * row_count
    selector = (script[:, None] == jnp.arange(groups, dtype=jnp.int32)[None, :]).astype(jnp.float32)
    added = jnp.dot(selector.astype(jnp.bfloat16), script_table, preferred_element_type=jnp.float32)
    hidden = (patches.astype(jnp.float32) + added[:, None, :]).reshape(tokens, model_width)
    normed_one, inverse_one = normalize(hidden)
    inputs_one = (normed_one * gain_one + bias_one).astype(jnp.bfloat16)
    joint_bias = jnp.concatenate([query_bias, jnp.zeros_like(query_bias), value_bias])
    projected = (
        jnp.dot(inputs_one, qkv_weight, preferred_element_type=jnp.float32) + joint_bias
    ).astype(jnp.bfloat16)
    projected = projected.reshape(strips, row_count, 3, model_width)
    head_blocks = lax.all_to_all(projected, "seq", split_axis=3, concat_axis=1, tiled=True)
    mixed_heads, log_totals = lax.map(attend_forward, (head_blocks, lengths))
    mixed = lax.all_to_all(mixed_heads, "seq", split_axis=1, concat_axis=2, tiled=True).reshape(
        tokens, model_width
    )
    attended = hidden + jnp.dot(mixed, out_weight, preferred_element_type=jnp.float32) + out_bias
    normed_two, inverse_two = normalize(attended)
    inputs_two = (normed_two * gain_two + bias_two).astype(jnp.bfloat16)
    upper = jnp.dot(inputs_two, up_weight, preferred_element_type=jnp.float32) + up_bias
    active = jax.nn.gelu(upper, approximate=False).astype(jnp.bfloat16)
    result = attended + jnp.dot(active, down_weight, preferred_element_type=jnp.float32) + down_bias
    layer_out = result.astype(jnp.bfloat16).reshape(strips, row_count, model_width)
    grad_result = cotangent.reshape(tokens, model_width)
    grad_float = grad_result.astype(jnp.float32)
    grad_down_weight = weight_grad(active, grad_result)
    grad_down_bias = jnp.sum(grad_float, axis=0)
    grad_upper = (input_grad(grad_result, down_weight) * gelu_slope(upper)).astype(jnp.bfloat16)
    grad_up_weight = weight_grad(inputs_two, grad_upper)
    grad_up_bias = jnp.sum(grad_upper.astype(jnp.float32), axis=0)
    grad_inputs_two = input_grad(grad_upper, up_weight)
    grad_gain_two = jnp.sum(grad_inputs_two * normed_two, axis=0)
    grad_bias_two = jnp.sum(grad_inputs_two, axis=0)
    grad_attended = grad_float + norm_back(grad_inputs_two, gain_two, normed_two, inverse_two)
    grad_branch = grad_attended.astype(jnp.bfloat16)
    grad_out_weight = weight_grad(mixed, grad_branch)
    grad_out_bias = jnp.sum(grad_branch.astype(jnp.float32), axis=0)
    grad_mixed = (
        input_grad(grad_branch, out_weight)
        .astype(jnp.bfloat16)
        .reshape(strips, row_count, model_width)
    )
    grad_mixed_heads = lax.all_to_all(grad_mixed, "seq", split_axis=2, concat_axis=1, tiled=True)
    grad_heads = lax.map(attend_backward, (head_blocks, log_totals, grad_mixed_heads, lengths))
    grad_projected = lax.all_to_all(
        grad_heads, "seq", split_axis=1, concat_axis=3, tiled=True
    ).reshape(tokens, 3 * model_width)
    grad_qkv = weight_grad(inputs_one, grad_projected)
    grad_bias_rows = jnp.sum(grad_projected.astype(jnp.float32), axis=0)
    grad_query_bias = grad_bias_rows[:model_width]
    grad_value_bias = grad_bias_rows[2 * model_width :]
    grad_inputs_one = input_grad(grad_projected, qkv_weight)
    grad_gain_one = jnp.sum(grad_inputs_one * normed_one, axis=0)
    grad_bias_one = jnp.sum(grad_inputs_one, axis=0)
    grad_hidden = grad_attended + norm_back(grad_inputs_one, gain_one, normed_one, inverse_one)
    grad_patches = grad_hidden.astype(jnp.bfloat16).reshape(strips, row_count, model_width)
    per_strip = jnp.sum(grad_hidden.reshape(strips, row_count, model_width), axis=1)
    grad_table = jnp.dot(per_strip.T, selector, precision=lax.Precision.HIGHEST)
    summed = (
        lax.psum_scatter(grad_table, ("strip", "seq"), scatter_dimension=0, tiled=True),
        lax.psum_scatter(grad_gain_one, ("strip", "seq"), scatter_dimension=0, tiled=True),
        lax.psum_scatter(grad_bias_one, ("strip", "seq"), scatter_dimension=0, tiled=True),
        lax.psum_scatter(grad_qkv, ("strip", "seq"), scatter_dimension=0, tiled=True),
        lax.psum_scatter(grad_query_bias, ("strip", "seq"), scatter_dimension=0, tiled=True),
        lax.psum_scatter(grad_value_bias, ("strip", "seq"), scatter_dimension=0, tiled=True),
        lax.psum_scatter(grad_out_weight, ("strip", "seq"), scatter_dimension=0, tiled=True),
        lax.psum_scatter(grad_out_bias, ("strip", "seq"), scatter_dimension=0, tiled=True),
        lax.psum_scatter(grad_gain_two, ("strip", "seq"), scatter_dimension=0, tiled=True),
        lax.psum_scatter(grad_bias_two, ("strip", "seq"), scatter_dimension=0, tiled=True),
        lax.psum_scatter(grad_up_weight, ("strip", "seq"), scatter_dimension=0, tiled=True),
        lax.psum_scatter(grad_up_bias, ("strip", "seq"), scatter_dimension=0, tiled=True),
        lax.psum_scatter(grad_down_weight, ("strip", "seq"), scatter_dimension=0, tiled=True),
        lax.psum_scatter(grad_down_bias, ("strip", "seq"), scatter_dimension=0, tiled=True),
    )
    return (
        layer_out,
        grad_patches,
        summed[0],
        summed[1],
        summed[2],
        summed[3],
        summed[4],
        summed[5],
        summed[6],
        summed[7],
        summed[8],
        summed[9],
        summed[10],
        summed[11],
        summed[12],
        summed[13],
    )


def solution(mesh):
    placed = (
        P("strip", "seq", None),
        P("strip"),
        P("strip"),
        P(),
        P(),
        P(),
        P(),
        P(),
        P(),
        P(),
        P(),
        P(),
        P(),
        P(),
        P(),
        P(),
        P(),
        P("strip", "seq", None),
    )
    return jax.shard_map(
        local,
        mesh=mesh,
        in_specs=placed,
        out_specs=(
            P("strip", "seq", None),
            P("strip", "seq", None),
            P(("strip", "seq"), None),
            P(("strip", "seq")),
            P(("strip", "seq")),
            P(("strip", "seq"), None),
            P(("strip", "seq")),
            P(("strip", "seq")),
            P(("strip", "seq"), None),
            P(("strip", "seq")),
            P(("strip", "seq")),
            P(("strip", "seq")),
            P(("strip", "seq"), None),
            P(("strip", "seq")),
            P(("strip", "seq"), None),
            P(("strip", "seq")),
        ),
        check_vma=False,
    )
```

profile of v0, /device:TPU:0, one launch (start us, length us, event | category | flops | bytes accessed | tf_op | source)
XLA Modules:
  0.0 786.1 jit_solution(12835965384405361480)
XLA Ops:
  10.6 2.6 multiply_reduce_fusion.6
  17.2 3.0 add_convert_fusion.1
  21.7 2.8 reshape.248
  25.4 5.2 add_convert_fusion
  30.5 7.7 reshape.249
  38.3 10.1 %copy.125 = bf16[4,134,3,768]{1,0,2,3:T(4,128)(2,1)} copy(bf16[4,134,3,768]{3,2,1,0:T(4,128)(2,1)} %reshape.249) | data formatting | bytes 4939776 | tf_op jit(solution)/shard_map/reshape | solution.py:125
  48.4 5.1 all-to-all-start
  53.5 54.5 %all-to-all-done = bf16[4,134,3,768]{1,0,2,3:T(4,128)(2,1)} async-done(((bf16[4,134,3,768]{1,0,2,3:T(4,128)(2,1)}), bf16[4,134,3,768]{1,0,2,3:T(4,128)(2,1)}, u32[]{:S(2)}, u32[]{:S(2)}) %all-to-all-start) | async-done | bytes 2469920 | tf_op jit(solution)/shard_map/all_to_all | solution.py:126
  108.0 8.1 %copy.158 = bf16[4,4,134,3,192]{2,1,4,3,0:T(4,128)(2,1)} copy(bf16[4,4,134,3,192]{2,0,3,4,1:T(4,128)(2,1)} %bitcast.23) | data formatting | bytes 4939776 | tf_op jit(solution)/shard_map/while | solution.py:127
  116.2 8.7 %reshape.260 = bf16[4,536,3,192]{1,3,2,0:T(8,128)(2,1)} reshape(bf16[4,4,134,3,192]{2,1,4,3,0:T(4,128)(2,1)} %copy.158) | data formatting | bytes 4939776 | tf_op jit(solution)/shard_map/while | solution.py:127
  124.9 27.9 %while.22 = (s32[]{:T(128)}, bf16[4,536,192]{1,2,0:T(8,128)(2,1)}, f32[4,3,536]{2,1,0:T(4,128)}, bf16[4,536,3,192]{1,3,2,0:T(8,128)(2,1)}, s32[4]{0:T(128)S(1)}, /*index=5*/s32[]{:T(128)}) while((s32[]{:T(128)}, bf16[4,536,192]{1,2,0:T(8,128)(2,1)}, f32[4,3,536]{2,1,0:T(4,128)}, bf16[4,536,3,192]{1,3,2,0:T(8,128)(2,1)}, s32[4]{0:T(128)S(1)}, ...), condition=%wide.region_5.6_spmd, body=%wide.region_2.5_spmd.sunk | while | flops 231087808 | bytes 14145945 | solution.py:127
  152.8 3.3 copy.129
  156.0 4.5 all-to-all-start.1
  162.7 2.3 reshape.252
  164.9 10.6 %all-to-all-done.1 = bf16[4,536,192]{2,0,1:T(4,128)(2,1)} async-done(((bf16[4,536,192]{2,0,1:T(4,128)(2,1)}), bf16[4,536,192]{2,0,1:T(4,128)(2,1)}, u32[]{:S(2)}, u32[]{:S(2)}) %all-to-all-start.1) | async-done | bytes 823328 | tf_op jit(solution)/shard_map/all_to_all | solution.py:128
  178.3 3.1 reshape.250
  181.4 3.1 fusion.51
  184.9 20.2 %fusion.19 = (bf16[536,3072]{1,0:T(8,128)(2,1)}, f32[536,3072]{1,0:T(8,128)S(1)}) fusion(f32[3072]{0:T(1024)S(1)} %copy-done.19, bf16[768,3072]{1,0:T(8,128)(2,1)} %param.35, f32[536,768]{1,0:T(8,128)S(1)} %get-tuple-element.262, f32[768]{0:T(1024)S(1)} %copy-done.9, f32[768]{0:T(1024)S(1)} %copy-done.8, f32[536]{0:T(1024)S(1)} %add_rsqrt_fusion.1, ...), kind=kOutput, calls=%fused_computation.36 | convolution fusion | flops 2639898624 | bytes 16267456 | tf_op jit(solution)/shard_map/dot_general | solution.py:134
  205.2 5.9 convert_reduce_fusion.1
  211.0 3.7 multiply_reduce_fusion.1
  221.2 3.5 copy.133
  224.7 4.4 all-to-all-start.2
  229.2 4.2 fusion.42
  233.4 15.8 %all-to-all-done.2 = bf16[4,134,768]{1,0,2:T(4,128)(2,1)} async-done(((bf16[4,134,768]{1,0,2:T(4,128)(2,1)}), bf16[4,134,768]{1,0,2:T(4,128)(2,1)}, u32[]{:S(2)}, u32[]{:S(2)}) %all-to-all-start.2) | async-done | bytes 823328 | tf_op jit(solution)/shard_map/all_to_all | solution.py:157
  249.2 3.9 copy.154
  253.1 4.1 reshape.257
  257.1 45.3 %while.23 = (s32[]{:T(128)}, bf16[4,536,3,192]{1,3,2,0:T(8,128)(2,1)}, bf16[4,536,3,192]{1,3,2,0:T(8,128)(2,1)}, s32[4]{0:T(128)}, f32[4,3,536]{2,1,0:T(4,128)}, /*index=5*/bf16[4,536,192]{1,2,0:T(8,128)(2,1)}, s32[]{:T(128)}) while((s32[]{:T(128)}, bf16[4,536,3,192]{1,3,2,0:T(8,128)(2,1)}, bf16[4,536,3,192]{1,3,2,0:T(8,128)(2,1)}, ...), condition=%wide.region_12.13_spmd, body=%wide.region_10.12_spmd.sunk | while | flops 566902528 | bytes 32199044 | solution.py:158
  302.4 7.7 copy.138
  310.0 4.7 all-to-all-start.3
  319.2 34.6 %all-to-all-done.3 = bf16[4,536,3,192]{3,0,2,1:T(4,128)(2,1)} async-done(((bf16[4,536,3,192]{3,0,2,1:T(4,128)(2,1)}), bf16[4,536,3,192]{3,0,2,1:T(4,128)(2,1)}, u32[]{:S(2)}, u32[]{:S(2)}) %all-to-all-start.3) | async-done | bytes 2469920 | tf_op jit(solution)/shard_map/all_to_all | solution.py:159
  353.8 2.4 copy.167
  356.3 3.0 copy.140
  359.2 6.8 reshape.254
  366.0 7.8 fusion.53
  373.9 10.2 %fusion.45 = f32[768,3072]{1,0:T(8,128)} fusion(bf16[536,3072]{1,0:T(8,128)(2,1)} %copy-done.6, f32[536,768]{1,0:T(8,128)} %copy-done.3, f32[768]{0:T(1024)S(1)} %copy-done.9, f32[768]{0:T(1024)S(1)} %copy-done.8, f32[536]{0:T(1024)S(1)} %add_rsqrt_fusion.1, f32[536]{0:T(1024)S(1)} %broadcast_multiply_fusion.5), kind=kOutput, calls=%fused_computation.107 | convolution fusion | flops 2531223552 | bytes 14387392 | tf_op jit(solution)/shard_map/dot_general | solution.py:26
  384.4 9.9 %fusion.54 = f32[3072,768]{1,0:T(8,128)} fusion(bf16[536,3072]{1,0:T(8,128)(2,1)} %get-tuple-element.263, bf16[536,768]{1,0:T(8,128)(2,1)} %reshape.252), kind=kOutput, calls=%fused_computation.116 | convolution fusion | flops 2529165312 | bytes 13553664 | tf_op jit(solution)/shard_map/dot_general | solution.py:26
  395.9 7.7 add_convert_fusion.2
  403.6 2.3 reshape.251
  405.9 2.4 copy.143
  408.3 5.5 multiply_reduce_fusion.2
  415.9 2.8 reshape.256
  420.9 2.4 convert_reduce_fusion
  426.3 44.2 %all-reduce.10 = (f32[768,4]{0,1:T(4,128)}, f32[768]{0:T(1024)}, f32[768]{0:T(1024)}, f32[768]{0:T(1024)}, f32[768]{0:T(1024)}, /*index=5*/f32[768]{0:T(1024)}, ...) all-reduce(f32[768,4]{0,1:T(4,128)} %fusion.38, ...), channel_id=2, replica_groups=mesh['strip'=8,'seq'=4] {'strip','seq'}, use_global_device_ids=true, to_apply=%region_16.17.clone | all-reduce | flops 12288 | bytes 98304
  480.6 2.3 reshape.255
  482.9 2.4 copy.144
  487.8 8.3 %reduce-scatter.6.cloned.1.call-done = f32[24,2304]{1,0:T(8,128)} async-done(((f32[768,2304]{1,0:T(8,128)}), f32[24,2304]{1,0:T(8,128)}) %reduce-scatter.6.cloned.1.call-update) | async-done | bytes 221200 | tf_op jit(solution)/shard_map/reduce_scatter | solution.py:177
  496.1 141.7 %reduce-scatter.10.cloned.1.call-done = f32[24,3072]{1,0:T(8,128)} async-done(((f32[768,3072]{1,0:T(8,128)}), f32[24,3072]{1,0:T(8,128)}) %reduce-scatter.10.cloned.1.call-update) | async-done | bytes 294928 | tf_op jit(solution)/shard_map/reduce_scatter | solution.py:184
  637.8 141.5 %reduce-scatter.12.cloned.1.call-done = f32[96,768]{1,0:T(8,128)} async-done(((f32[3072,768]{1,0:T(8,128)}), f32[96,768]{1,0:T(8,128)}) %reduce-scatter.12.cloned.1.call-update) | async-done | bytes 294928 | tf_op jit(solution)/shard_map/reduce_scatter | solution.py:186
  (204 shorter events, 120.8 us)
Async XLA Ops:
  7.2 18.2 %copy-start = (bf16[768,2304]{1,0:T(8,128)(2,1)S(1)}, bf16[768,2304]{1,0:T(8,128)(2,1)}, u32[]{:S(2)}) copy-start(bf16[768,2304]{1,0:T(8,128)(2,1)} %param.28) | copy-start | bytes 10616836
  9.9 0.6 copy-start.7
  20.2 4.3 copy-start.17
  20.2 5.2 copy-start.10
  24.6 6.0 copy-start.13
  24.6 5.9 copy-start.15
  48.4 59.6 %all-to-all-start = ((bf16[4,134,3,768]{1,0,2,3:T(4,128)(2,1)}), bf16[4,134,3,768]{1,0,2,3:T(4,128)(2,1)}, u32[]{:S(2)}, u32[]{:S(2)}) async-start(bf16[4,134,3,768]{1,0,2,3:T(4,128)(2,1)} %copy.125), calls=%async_computation | async-start | bytes 9437184 | tf_op jit(solution)/shard_map/all_to_all | solution.py:126
  116.1 8.7 %copy-start.21 = (s32[4]{0:T(128)S(1)}, s32[4]{0:T(128)}, u32[]{:S(2)}) copy-start(s32[4]{0:T(128)} %param.23) | copy-start | bytes 52
  156.0 19.5 %all-to-all-start.1 = ((bf16[4,536,192]{2,0,1:T(4,128)(2,1)}), bf16[4,536,192]{2,0,1:T(4,128)(2,1)}, u32[]{:S(2)}, u32[]{:S(2)}) async-start(bf16[4,536,192]{2,0,1:T(4,128)(2,1)} %copy.129), calls=%async_computation.1 | async-start | bytes 2195456 | tf_op jit(solution)/shard_map/all_to_all | solution.py:128
  164.9 16.4 %copy-start.20 = (f32[768]{0:T(1024)S(1)}, f32[768]{0:T(1024)}, u32[]{:S(2)}) copy-start(f32[768]{0:T(1024)} %param.32) | copy-start | bytes 9220
  181.3 3.5 copy-start.8
  181.3 3.5 copy-start.9
  181.3 3.5 copy-start.19
  181.4 23.8 %slice-start.2 = ((s8[4718592]{0:T(1024)(128)(4,1)}), s8[4194304]{0:T(1024)(128)(4,1)S(1)}, s32[]{:S(2)}) async-start(s8[4718592]{0:T(1024)(128)(4,1)} %bitcast.162), calls=%async_computation.14 | async-start | bytes 8388608
  181.4 29.7 %slice-start = ((s8[4718592]{0:T(1024)(128)(4,1)}), s8[4194304]{0:T(1024)(128)(4,1)S(1)}, s32[]{:S(2)}) async-start(s8[4718592]{0:T(1024)(128)(4,1)} %bitcast.160), calls=%async_computation.12 | async-start | bytes 8388608
  184.5 30.2 %copy-start.3 = (f32[536,768]{1,0:T(8,128)}, f32[536,768]{1,0:T(8,128)S(1)}, u32[]{:S(2)}) copy-start(f32[536,768]{1,0:T(8,128)S(1)} %get-tuple-element.262) | copy-start | bytes 4939780
  184.9 20.2 %copy-start.5 = (bf16[536,768]{1,0:T(8,128)(2,1)S(1)}, bf16[536,768]{1,0:T(8,128)(2,1)}, u32[]{:S(2)}) copy-start(bf16[536,768]{1,0:T(8,128)(2,1)} %reshape.252) | copy-start | bytes 2469892
  184.9 20.2 %slice-start.3 = ((s8[4718592]{0:T(1024)(128)(4,1)}), s8[524288]{0:T(1024)(128)(4,1)S(1)}, s32[]{:S(2)}) async-start(s8[4718592]{0:T(1024)(128)(4,1)} %bitcast.162), calls=%async_computation.15 | async-start | bytes 1048576
  184.9 26.1 %slice-start.1 = ((s8[4718592]{0:T(1024)(128)(4,1)}), s8[524288]{0:T(1024)(128)(4,1)S(1)}, s32[]{:S(2)}) async-start(s8[4718592]{0:T(1024)(128)(4,1)} %bitcast.160), calls=%async_computation.13 | async-start | bytes 1048576
  211.0 3.7 copy-start.6
  214.7 2.5 copy-start.18
  216.0 1.2 copy-start.1
  224.7 24.5 %all-to-all-start.2 = ((bf16[4,134,768]{1,0,2:T(4,128)(2,1)}), bf16[4,134,768]{1,0,2:T(4,128)(2,1)}, u32[]{:S(2)}, u32[]{:S(2)}) async-start(bf16[4,134,768]{1,0,2:T(4,128)(2,1)} %copy.133), calls=%async_computation.2 | async-start | bytes 3145728 | tf_op jit(solution)/shard_map/all_to_all | solution.py:157
  229.1 258.7 %reduce-scatter.8.cloned.1.call-start = ((), (), s32[]{:S(2)}) async-start(), calls=%async_computation.9 | async-start | bytes 2433024 | tf_op jit(solution)/shard_map/reduce_scatter | solution.py:180
  258.3 1.6 copy-start.22
  269.6 1.6 copy-start.22
  280.9 1.6 copy-start.22
  292.2 1.6 copy-start.22
  310.0 43.8 %all-to-all-start.3 = ((bf16[4,536,3,192]{3,0,2,1:T(4,128)(2,1)}), bf16[4,536,3,192]{3,0,2,1:T(4,128)(2,1)}, u32[]{:S(2)}, u32[]{:S(2)}) async-start(bf16[4,536,3,192]{3,0,2,1:T(4,128)(2,1)} %copy.138), calls=%async_computation.3 | async-start | bytes 6586368 | tf_op jit(solution)/shard_map/all_to_all | solution.py:159
  314.8 181.3 %reduce-scatter.6.cloned.1.call-start = ((), (), s32[]{:S(2)}) async-start(), calls=%async_computation.8 | async-start | bytes 7299072 | tf_op jit(solution)/shard_map/reduce_scatter | solution.py:177
  373.9 263.9 %reduce-scatter.10.cloned.1.call-start = ((), (), s32[]{:S(2)}) async-start(), calls=%async_computation.10 | async-start | bytes 9732096 | tf_op jit(solution)/shard_map/reduce_scatter | solution.py:184
  384.1 395.2 %reduce-scatter.12.cloned.1.call-start = ((), (), s32[]{:S(2)}) async-start(), calls=%async_computation.11 | async-start | bytes 9732096 | tf_op jit(solution)/shard_map/reduce_scatter | solution.py:186
  395.9 12.5 %copy-start.11 = (f32[768]{0:T(1024)S(1)}, f32[768]{0:T(1024)}, u32[]{:S(2)}) copy-start(f32[768]{0:T(1024)} %param.26) | copy-start | bytes 9220
  395.9 12.5 %copy-start.14 = (f32[536]{0:T(1024)S(1)}, f32[536]{0:T(1024)}, u32[]{:S(2)}) copy-start(f32[536]{0:T(1024)} %copy-done.13) | copy-start | bytes 6436
  395.9 12.4 %copy-start.16 = (f32[536]{0:T(1024)S(1)}, f32[536]{0:T(1024)}, u32[]{:S(2)}) copy-start(f32[536]{0:T(1024)} %copy-done.15) | copy-start | bytes 6436
  408.3 5.6 copy-start.2
  408.3 5.6 copy-start.4
  418.8 7.6 copy-start.12
Sparse Core Ops, SparseCore 0:
  235.8 102.1 reduce-scatter.7
  374.0 122.0 reduce-scatter.5
  502.6 135.1 reduce-scatter.9
  644.1 135.1 reduce-scatter.11
where the time goes:
time: 795 us; the launch traced here: 786 us
  waiting for transfers between devices  407 us (51%)
  local copies, waits for them, and re-layouts  146 us (18%)
  matrix products  116 us (15%)
  blocking collectives  44.2 us (6%)
  other arithmetic  39.8 us (5%)
  starting transfers between devices  19 us (2%)
  between operations  14.3 us (2%)
    reduce_scatter x1, waiting for transfers between devices, local(): lax.psum_scatter(grad_up_weight, ('strip', 'seq'), scatter_dimension=0, t...  142 us
    reduce_scatter x1, waiting for transfers between devices, local(): lax.psum_scatter(grad_down_weight, ('strip', 'seq'), scatter_dimension=0,...  141 us
    all_to_all x1, waiting for transfers between devices, local(): lax.all_to_all(projected, 'seq', split_axis=3, concat_axis=1, tiled=True)  54.5 us
    unnamed x1, blocking collectives  44.2 us
    all_to_all x1, waiting for transfers between devices, local(): lax.all_to_all(grad_heads, 'seq', split_axis=1, concat_axis=3, tiled=True)  34.6 us
    dot_general x4, matrix products, weight_grad(): lax.dot_general(inputs, upstream, (((0,), (0,)), ((), ())), preferred_ele...  32.1 us
    unnamed x67, local copies, waits for them, and re-layouts  24 us
    dot_general x1, matrix products, local(): jnp.dot(inputs_two, up_weight, preferred_element_type=jnp.float32) + up_bias  20.2 us
  transfers between devices with their start and end apart: 8, of which 7 were waited for; matrix products, arithmetic and copies ran while one was open for 21% of the time, Pallas kernels for 0%

commit v1 on v0

--- a/solution.py
+++ b/solution.py
@@ -1,3 +1,4 @@
+import functools
 import jax
 import jax.numpy as jnp
 from jax import lax
@@ -5,6 +6,19 @@
 
 HD = 64
 epsilon = 1e-12
+
+
+def lift_the_meshes(v0, axis_tag):
+    w_next = jnp.concatenate(
+        lax.all_to_all(
+            jnp.stack(jnp.split(v0, lax.axis_size(axis_tag), 2), axis=0), axis_tag, 0, 0
+        ),
+        1,
+    )
+    return w_next
+
+
+_meet_modes = functools.partial(lift_the_meshes, axis_tag="seq")
 
 
 def normalize(hidden):
@@ -154,7 +168,7 @@
         .astype(jnp.bfloat16)
         .reshape(strips, row_count, model_width)
     )
-    grad_mixed_heads = lax.all_to_all(grad_mixed, "seq", split_axis=2, concat_axis=1, tiled=True)
+    grad_mixed_heads = _meet_modes(grad_mixed)
     grad_heads = lax.map(attend_backward, (head_blocks, log_totals, grad_mixed_heads, lengths))
     grad_projected = lax.all_to_all(
         grad_heads, "seq", split_axis=1, concat_axis=3, tiled=True

time: 795 us -> 786 us (0.989)
    unnamed x67 -> x69, local copies, waits for them, and re-layouts: 24 us -> 24 us
  transfers between devices with their start and end apart: 8 -> 8, of which waited for: 7 -> 7; matrix products, arithmetic and copies ran while one was open for 21% -> 20% of each run, Pallas kernels for 0% -> 0%
where the time goes in v1:
time: 786 us; the launch traced here: 777 us
  waiting for transfers between devices  404 us (51%)
  local copies, waits for them, and re-layouts  141 us (18%)
  matrix products  115 us (15%)
  blocking collectives  43.3 us (6%)
  other arithmetic  40.1 us (5%)
  starting transfers between devices  18.9 us (2%)
  between operations  14.3 us (2%)
    reduce_scatter x1, waiting for transfers between devices, local(): lax.psum_scatter(grad_up_weight, ('strip', 'seq'), scatter_dimension=0, t...  142 us
    reduce_scatter x1, waiting for transfers between devices, local(): lax.psum_scatter(grad_down_weight, ('strip', 'seq'), scatter_dimension=0,...  141 us
    all_to_all x1, waiting for transfers between devices, local(): lax.all_to_all(projected, 'seq', split_axis=3, concat_axis=1, tiled=True)  54.5 us
    unnamed x1, blocking collectives  43.3 us
    all_to_all x1, waiting for transfers between devices, local(): lax.all_to_all(grad_heads, 'seq', split_axis=1, concat_axis=3, tiled=True)  36.6 us
    dot_general x4, matrix products, weight_grad(): lax.dot_general(inputs, upstream, (((0,), (0,)), ((), ())), preferred_ele...  32.1 us
    unnamed x69, local copies, waits for them, and re-layouts  24 us
    dot_general x1, matrix products, local(): jnp.dot(inputs_two, up_weight, preferred_element_type=jnp.float32) + up_bias  20.2 us
  transfers between devices with their start and end apart: 8, of which 7 were waited for; matrix products, arithmetic and copies ran while one was open for 20% of the time, Pallas kernels for 0%

profile of v1, /device:TPU:0, one launch (start us, length us, event | category | flops | bytes accessed | tf_op | source)
XLA Modules:
  0.0 777.2 jit_solution(4830970862818303687)
XLA Ops:
  10.6 2.6 multiply_reduce_fusion.6
  17.2 3.0 add_convert_fusion.1
  21.7 2.8 reshape.254
  25.4 5.2 add_convert_fusion
  30.5 7.7 reshape.255
  38.3 10.1 %copy.123 = bf16[4,134,3,768]{1,0,2,3:T(4,128)(2,1)} copy(bf16[4,134,3,768]{3,2,1,0:T(4,128)(2,1)} %reshape.255) | data formatting | bytes 4939776 | tf_op jit(solution)/shard_map/reshape | solution.py:139
  48.4 5.1 all-to-all-start
  53.5 54.5 %all-to-all-done = bf16[4,134,3,768]{1,0,2,3:T(4,128)(2,1)} async-done(((bf16[4,134,3,768]{1,0,2,3:T(4,128)(2,1)}), bf16[4,134,3,768]{1,0,2,3:T(4,128)(2,1)}, u32[]{:S(2)}, u32[]{:S(2)}) %all-to-all-start) | async-done | bytes 2469920 | tf_op jit(solution)/shard_map/all_to_all | solution.py:140
  108.0 8.1 %copy.154 = bf16[4,4,134,3,192]{2,1,4,3,0:T(4,128)(2,1)} copy(bf16[4,4,134,3,192]{2,0,3,4,1:T(4,128)(2,1)} %bitcast.23) | data formatting | bytes 4939776 | tf_op jit(solution)/shard_map/while | solution.py:141
  116.2 8.7 %reshape.267 = bf16[4,536,3,192]{1,3,2,0:T(8,128)(2,1)} reshape(bf16[4,4,134,3,192]{2,1,4,3,0:T(4,128)(2,1)} %copy.154) | data formatting | bytes 4939776 | tf_op jit(solution)/shard_map/while | solution.py:141
  124.9 27.9 %while.22 = (s32[]{:T(128)}, bf16[4,536,192]{1,2,0:T(8,128)(2,1)}, f32[4,3,536]{2,1,0:T(4,128)}, bf16[4,536,3,192]{1,3,2,0:T(8,128)(2,1)}, s32[4]{0:T(128)S(1)}, /*index=5*/s32[]{:T(128)}) while((s32[]{:T(128)}, bf16[4,536,192]{1,2,0:T(8,128)(2,1)}, f32[4,3,536]{2,1,0:T(4,128)}, bf16[4,536,3,192]{1,3,2,0:T(8,128)(2,1)}, s32[4]{0:T(128)S(1)}, ...), condition=%wide.region_5.6_spmd, body=%wide.region_2.5_spmd.sunk | while | flops 231087808 | bytes 14145945 | solution.py:141
  152.8 3.3 copy.127
  156.0 4.5 all-to-all-start.1
  162.7 2.3 reshape.258
  164.9 10.6 %all-to-all-done.1 = bf16[4,536,192]{2,0,1:T(4,128)(2,1)} async-done(((bf16[4,536,192]{2,0,1:T(4,128)(2,1)}), bf16[4,536,192]{2,0,1:T(4,128)(2,1)}, u32[]{:S(2)}, u32[]{:S(2)}) %all-to-all-start.1) | async-done | bytes 823328 | tf_op jit(solution)/shard_map/all_to_all | solution.py:142
  178.3 3.1 reshape.256
  181.4 3.1 fusion.51
  184.9 20.2 %fusion.19 = (bf16[536,3072]{1,0:T(8,128)(2,1)}, f32[536,3072]{1,0:T(8,128)S(1)}) fusion(f32[3072]{0:T(1024)S(1)} %copy-done.19, bf16[768,3072]{1,0:T(8,128)(2,1)} %param.35, f32[536,768]{1,0:T(8,128)S(1)} %get-tuple-element.266, f32[768]{0:T(1024)S(1)} %copy-done.9, f32[768]{0:T(1024)S(1)} %copy-done.8, f32[536]{0:T(1024)S(1)} %add_rsqrt_fusion.1, ...), kind=kOutput, calls=%fused_computation.36 | convolution fusion | flops 2639898624 | bytes 16267456 | tf_op jit(solution)/shard_map/dot_general | solution.py:148
  205.2 5.7 convert_reduce_fusion.1
  210.9 3.7 multiply_reduce_fusion.1
  218.8 2.3 reshape.259
  224.3 4.3 all-to-all-start.2
  228.6 4.2 fusion.42
  232.9 10.7 %all-to-all-done.2 = bf16[4,4,134,192]{3,1,2,0:T(4,128)(2,1)} async-done(((bf16[4,4,134,192]{3,1,2,0:T(4,128)(2,1)}), bf16[4,4,134,192]{3,1,2,0:T(4,128)(2,1)}, u32[]{:S(2)}, u32[]{:S(2)}) %all-to-all-start.2) | async-done | bytes 823328 | tf_op jit(solution)/shard_map/all_to_all | solution.py:13
  243.6 3.6 copy.134
  247.2 45.4 %while.23 = (s32[]{:T(128)}, bf16[4,536,3,192]{1,3,2,0:T(8,128)(2,1)}, bf16[4,536,3,192]{1,3,2,0:T(8,128)(2,1)}, s32[4]{0:T(128)}, f32[4,3,536]{2,1,0:T(4,128)}, /*index=5*/bf16[4,536,192]{1,2,0:T(8,128)(2,1)}, s32[]{:T(128)}) while((s32[]{:T(128)}, bf16[4,536,3,192]{1,3,2,0:T(8,128)(2,1)}, bf16[4,536,3,192]{1,3,2,0:T(8,128)(2,1)}, ...), condition=%wide.region_12.13_spmd, body=%wide.region_10.12_spmd.sunk | while | flops 566902528 | bytes 32199044 | solution.py:172
  292.6 7.7 copy.135
  300.3 4.7 all-to-all-start.3
  307.2 2.3 convert_element_type.94
  309.5 36.6 %all-to-all-done.3 = bf16[4,536,3,192]{3,0,2,1:T(4,128)(2,1)} async-done(((bf16[4,536,3,192]{3,0,2,1:T(4,128)(2,1)}), bf16[4,536,3,192]{3,0,2,1:T(4,128)(2,1)}, u32[]{:S(2)}, u32[]{:S(2)}) %all-to-all-start.3) | async-done | bytes 2469920 | tf_op jit(solution)/shard_map/all_to_all | solution.py:173
  346.1 2.4 copy.162
  348.5 3.0 copy.137
  351.4 6.8 reshape.262
  358.2 7.8 %fusion.53 = f32[768,2304]{1,0:T(8,128)} fusion(bf16[536,768]{1,0:T(8,128)(2,1)} %convert_element_type.94, bf16[536,2304]{1,0:T(8,128)(2,1)} %reshape.262), kind=kOutput, calls=%fused_computation.120 | convolution fusion | flops 1896873984 | bytes 10371072 | tf_op jit(solution)/shard_map/dot_general | solution.py:40
  366.1 10.2 %fusion.45 = f32[768,3072]{1,0:T(8,128)} fusion(bf16[536,3072]{1,0:T(8,128)(2,1)} %copy-done.6, f32[536,768]{1,0:T(8,128)} %copy-done.3, f32[768]{0:T(1024)S(1)} %copy-done.9, f32[768]{0:T(1024)S(1)} %copy-done.8, f32[536]{0:T(1024)S(1)} %add_rsqrt_fusion.1, f32[536]{0:T(1024)S(1)} %broadcast_multiply_fusion.5), kind=kOutput, calls=%fused_computation.112 | convolution fusion | flops 2531223552 | bytes 14387392 | tf_op jit(solution)/shard_map/dot_general | solution.py:40
  376.6 9.9 %fusion.54 = f32[3072,768]{1,0:T(8,128)} fusion(bf16[536,3072]{1,0:T(8,128)(2,1)} %get-tuple-element.267, bf16[536,768]{1,0:T(8,128)(2,1)} %reshape.258), kind=kOutput, calls=%fused_computation.121 | convolution fusion | flops 2529165312 | bytes 13553664 | tf_op jit(solution)/shard_map/dot_general | solution.py:40
  388.0 7.8 add_convert_fusion.2
  395.8 2.3 reshape.257
  398.1 2.4 copy.140
  400.5 5.5 multiply_reduce_fusion.2
  408.1 2.8 reshape.264
  413.1 2.4 convert_reduce_fusion
  418.5 43.3 %all-reduce.10 = (f32[768,4]{0,1:T(4,128)}, f32[768]{0:T(1024)}, f32[768]{0:T(1024)}, f32[768]{0:T(1024)}, f32[768]{0:T(1024)}, /*index=5*/f32[768]{0:T(1024)}, ...) all-reduce(f32[768,4]{0,1:T(4,128)} %fusion.38, ...), channel_id=2, replica_groups=mesh['strip'=8,'seq'=4] {'strip','seq'}, use_global_device_ids=true, to_apply=%region_16.17.clone | all-reduce | flops 12288 | bytes 98304
  471.9 2.3 reshape.263
  474.2 2.4 copy.141
  479.2 8.1 %reduce-scatter.6.cloned.1.call-done = f32[24,2304]{1,0:T(8,128)} async-done(((f32[768,2304]{1,0:T(8,128)}), f32[24,2304]{1,0:T(8,128)}) %reduce-scatter.6.cloned.1.call-update) | async-done | bytes 221200 | tf_op jit(solution)/shard_map/reduce_scatter | solution.py:191
  487.2 141.7 %reduce-scatter.10.cloned.1.call-done = f32[24,3072]{1,0:T(8,128)} async-done(((f32[768,3072]{1,0:T(8,128)}), f32[24,3072]{1,0:T(8,128)}) %reduce-scatter.10.cloned.1.call-update) | async-done | bytes 294928 | tf_op jit(solution)/shard_map/reduce_scatter | solution.py:198
  628.9 141.5 %reduce-scatter.12.cloned.1.call-done = f32[96,768]{1,0:T(8,128)} async-done(((f32[3072,768]{1,0:T(8,128)}), f32[96,768]{1,0:T(8,128)}) %reduce-scatter.12.cloned.1.call-update) | async-done | bytes 294928 | tf_op jit(solution)/shard_map/reduce_scatter | solution.py:200
  (207 shorter events, 119.6 us)
Async XLA Ops:
  7.2 18.2 %copy-start = (bf16[768,2304]{1,0:T(8,128)(2,1)S(1)}, bf16[768,2304]{1,0:T(8,128)(2,1)}, u32[]{:S(2)}) copy-start(bf16[768,2304]{1,0:T(8,128)(2,1)} %param.28) | copy-start | bytes 10616836
  9.9 0.6 copy-start.7
  20.2 4.3 copy-start.17
  20.2 5.2 copy-start.10
  24.6 6.0 copy-start.13
  24.6 5.9 copy-start.15
  48.4 59.6 %all-to-all-start = ((bf16[4,134,3,768]{1,0,2,3:T(4,128)(2,1)}), bf16[4,134,3,768]{1,0,2,3:T(4,128)(2,1)}, u32[]{:S(2)}, u32[]{:S(2)}) async-start(bf16[4,134,3,768]{1,0,2,3:T(4,128)(2,1)} %copy.123), calls=%async_computation | async-start | bytes 9437184 | tf_op jit(solution)/shard_map/all_to_all | solution.py:140
  116.1 8.7 %copy-start.22 = (s32[4]{0:T(128)S(1)}, s32[4]{0:T(128)}, u32[]{:S(2)}) copy-start(s32[4]{0:T(128)} %param.23) | copy-start | bytes 52
  156.0 19.5 %all-to-all-start.1 = ((bf16[4,536,192]{2,0,1:T(4,128)(2,1)}), bf16[4,536,192]{2,0,1:T(4,128)(2,1)}, u32[]{:S(2)}, u32[]{:S(2)}) async-start(bf16[4,536,192]{2,0,1:T(4,128)(2,1)} %copy.127), calls=%async_computation.1 | async-start | bytes 2195456 | tf_op jit(solution)/shard_map/all_to_all | solution.py:142
  164.9 16.4 %copy-start.20 = (f32[768]{0:T(1024)S(1)}, f32[768]{0:T(1024)}, u32[]{:S(2)}) copy-start(f32[768]{0:T(1024)} %param.32) | copy-start | bytes 9220
  181.3 3.5 copy-start.8
  181.3 3.5 copy-start.9
  181.3 3.5 copy-start.19
  181.4 23.8 %slice-start.2 = ((s8[4718592]{0:T(1024)(128)(4,1)}), s8[4194304]{0:T(1024)(128)(4,1)S(1)}, s32[]{:S(2)}) async-start(s8[4718592]{0:T(1024)(128)(4,1)} %bitcast.167), calls=%async_computation.14 | async-start | bytes 8388608
  181.4 29.5 %slice-start = ((s8[4718592]{0:T(1024)(128)(4,1)}), s8[4194304]{0:T(1024)(128)(4,1)S(1)}, s32[]{:S(2)}) async-start(s8[4718592]{0:T(1024)(128)(4,1)} %bitcast.165), calls=%async_computation.12 | async-start | bytes 8388608
  184.5 30.1 %copy-start.3 = (f32[536,768]{1,0:T(8,128)}, f32[536,768]{1,0:T(8,128)S(1)}, u32[]{:S(2)}) copy-start(f32[536,768]{1,0:T(8,128)S(1)} %get-tuple-element.266) | copy-start | bytes 4939780
  184.9 20.2 %copy-start.5 = (bf16[536,768]{1,0:T(8,128)(2,1)S(1)}, bf16[536,768]{1,0:T(8,128)(2,1)}, u32[]{:S(2)}) copy-start(bf16[536,768]{1,0:T(8,128)(2,1)} %reshape.258) | copy-start | bytes 2469892
  184.9 20.2 %slice-start.3 = ((s8[4718592]{0:T(1024)(128)(4,1)}), s8[524288]{0:T(1024)(128)(4,1)S(1)}, s32[]{:S(2)}) async-start(s8[4718592]{0:T(1024)(128)(4,1)} %bitcast.167), calls=%async_computation.15 | async-start | bytes 1048576
  184.9 26.0 %slice-start.1 = ((s8[4718592]{0:T(1024)(128)(4,1)}), s8[524288]{0:T(1024)(128)(4,1)S(1)}, s32[]{:S(2)}) async-start(s8[4718592]{0:T(1024)(128)(4,1)} %bitcast.165), calls=%async_computation.13 | async-start | bytes 1048576
  210.9 3.7 copy-start.6
  214.6 2.5 copy-start.18
  215.9 1.2 copy-start.1
  224.3 19.3 %all-to-all-start.2 = ((bf16[4,4,134,192]{3,1,2,0:T(4,128)(2,1)}), bf16[4,4,134,192]{3,1,2,0:T(4,128)(2,1)}, u32[]{:S(2)}, u32[]{:S(2)}) async-start(bf16[4,4,134,192]{3,1,2,0:T(4,128)(2,1)} %copy.131), calls=%async_computation.2 | async-start | bytes 2195456 | tf_op jit(solution)/shard_map/all_to_all | solution.py:13
  228.6 250.6 %reduce-scatter.8.cloned.1.call-start = ((), (), s32[]{:S(2)}) async-start(), calls=%async_computation.9 | async-start | bytes 2433024 | tf_op jit(solution)/shard_map/reduce_scatter | solution.py:194
  248.4 1.6 copy-start.23
  259.7 1.6 copy-start.23
  271.0 1.6 copy-start.23
  282.4 1.6 copy-start.23
  300.3 45.8 %all-to-all-start.3 = ((bf16[4,536,3,192]{3,0,2,1:T(4,128)(2,1)}), bf16[4,536,3,192]{3,0,2,1:T(4,128)(2,1)}, u32[]{:S(2)}, u32[]{:S(2)}) async-start(bf16[4,536,3,192]{3,0,2,1:T(4,128)(2,1)} %copy.135), calls=%async_computation.3 | async-start | bytes 6586368 | tf_op jit(solution)/shard_map/all_to_all | solution.py:173
  305.0 182.3 %reduce-scatter.6.cloned.1.call-start = ((), (), s32[]{:S(2)}) async-start(), calls=%async_computation.8 | async-start | bytes 7299072 | tf_op jit(solution)/shard_map/reduce_scatter | solution.py:191
  366.1 262.8 %reduce-scatter.10.cloned.1.call-start = ((), (), s32[]{:S(2)}) async-start(), calls=%async_computation.10 | async-start | bytes 9732096 | tf_op jit(solution)/shard_map/reduce_scatter | solution.py:198
  376.3 394.1 %reduce-scatter.12.cloned.1.call-start = ((), (), s32[]{:S(2)}) async-start(), calls=%async_computation.11 | async-start | bytes 9732096 | tf_op jit(solution)/shard_map/reduce_scatter | solution.py:200
  386.4 1.6 copy-start.21
  395.8 4.7 copy-start.11
  395.8 4.7 copy-start.14
  395.8 4.7 copy-start.16
  400.5 5.6 copy-start.2
  400.5 5.5 copy-start.4
  410.9 7.6 copy-start.12
Sparse Core Ops, SparseCore 0:
  235.3 102.7 reduce-scatter.7
  366.2 120.9 reduce-scatter.5
  493.7 135.1 reduce-scatter.9
  635.2 135.1 reduce-scatter.11
